TPU v7x, 32 devices: a 4x4x1 block of a 4x4x8 slice. The times are simulated.
32 devices in a mesh: dp: 1 (over z), tx: 4 (over y), ty: 8 (over x, core).
Axes of the slice: x: 4, y: 4, z: 1, core: 2. Of those that a mesh axis runs over, the one named last changes fastest.
The devices are a block of a 4x4x8 slice.
Arguments:
- x_in: bfloat16 [24, 576, 1024], P('dp', None, 'tx')
- ln1_gain: float32 [2, 1024], P(None, 'tx')
- ln1_bias: float32 [2, 1024], P(None, 'tx')
- w_q: bfloat16 [2, 1024, 16, 64], P(None, 'tx', 'ty')
- b_q: float32 [2, 16, 64], P(None, 'ty')
- w_k: bfloat16 [2, 1024, 16, 64], P(None, 'tx', 'ty')
- w_v: bfloat16 [2, 1024, 16, 64], P(None, 'tx', 'ty')
- b_v: float32 [2, 16, 64], P(None, 'ty')
- w_o: bfloat16 [2, 16, 64, 1024], P(None, 'ty', None, 'tx')
- b_o: float32 [2, 1024], P(None, 'tx')
- ln2_gain: float32 [2, 1024], P(None, 'tx')
- ln2_bias: float32 [2, 1024], P(None, 'tx')
- w_up: bfloat16 [2, 1024, 4096], P(None, 'tx', 'ty')
- b_up: float32 [2, 4096], P(None, 'ty')
- w_down: bfloat16 [2, 4096, 1024], P(None, 'ty', 'tx')
- b_down: float32 [2, 1024], P(None, 'tx')
Outputs:
- output: bfloat16 [24, 576, 1024], P('dp', None, 'tx')
All inputs are finite; a program needn't handle non-finite values.
Results may differ from a plain program's by a relative error of at most 0.02.
Values are sent between devices in bfloat16 or wider.
A program may use at most 768 MiB of HBM per device.

v0:
```python
import functools
import math

import jax
import jax.numpy as jnp
from jax import lax
from jax.experimental import pallas as pl
from jax.experimental.pallas import tpu as pltpu
from jax.sharding import PartitionSpec as P

EPS = 1e-6
F32, BF16 = jnp.float32, jnp.bfloat16
MESH = pl.DeviceIdType.MESH
CORES = 2
STEPS = {"xp": (1, 0), "xm": (-1, 0), "yp": (0, 1), "ym": (0, -1)}


def phases():
    out = [[] for _ in range(5)]
    for to, (sx, sy) in STEPS.items():
        s, turned = sx + sy, "B" if sx else "A"
        sign = "plus" if s > 0 else "minus"

        def along(d, e, sx=sx):
            return (d, e) if sx else (e, d)

        out[0] += [(to, (0, 0), "all", "all")]
        out[1] += [(to, along(-s, 0), "all", sign)] + [(to, along(0, e), turned, "all") for e in (-1, 1)]
        out[2] += [(to, along(0, 2), turned, "all")] + [(to, along(-s, e), turned, sign) for e in (-1, 1)]
        out[3] += [(to, along(-s, 2), turned, sign)]
    for part in out:
        n = len(part) // 4
        part[:] = [part[link * n + i] for i in range(n) for link in range(4)]
    for dx in range(-1, 3):
        for dy in range(-1, 3):
            out[abs(dx) + abs(dy)].append(("sib", (dx, dy), "all", "all"))
    return out


PHASES = phases()
SENT = ((5, 1), (5, 2), (5, 2), (5, 1), (1, 1))
BROUGHT = ((4, 1), (6, 1), (4, 1), (1, 1))
PASSED = ((4, 1), (8, 1), (4, 1))
BEFORE = "s10 s01 s20"
SLOTS = (
    ("l00 c00", "s11", "s30 l01", "s02 c01", "s21 l10", "s12", "s40 l02 c10 c02", "s31 s03 l11"),
    ("s22 l20 c20 c11", "s41 s13 l12", "s32 l21 c12", "c21", "s04", "s23 l30", "s42 l22 c30", "c22"),
    ("s05 s14", "s33 l31", "s15 c31", "", "s24 s43 l40 l32", "c32 c40", "s25 l50", "s34 l41 c50"),
    ("s35 l51 s44 l42", "c41 c51", "s45 l52", "", "", "", "c42 c52", ""),
)
RINGS = (((0,), (1,)), ((2, 3), (4, 5)), ((6,), (7,)))
PARTS = 4


def dot(a, b):
    return jnp.dot(a, b, preferred_element_type=F32)


def kernel(head, each, x_hbm, *refs):
    (wq_ref, wk_ref, wv_ref, wo_ref, wup_ref, wdown_ref, bq_ref, bv_ref, bup_ref,
     gain1_ref, shift1_ref, bo_ref, gain2_ref, shift2_ref, bdown_ref,
     out_ref, ga_ref, gu_ref, gd_ref,
     x_ref, h_ref, acc_ref, qkv_ref, o_ref, u_ref, own_a, own_u, own_d, wbuf_a, wbuf_u, wbuf_d, own_vec, own_bias, vecs, biases,
     send_sem, recv_sem, core_sem, in_sem, own_sem, load_sem, vec_send, vec_recv, bias_send, bias_recv,
     xin_send, xin_recv, o1_send, o1_recv, ring_send, ring_recv, ring_core) = refs
    layers, tys, txs = ga_ref.shape[:3]
    groups = 3 * layers
    owns, gathered = (own_a, own_u, own_d), (ga_ref, gu_ref, gd_ref)
    nx, ny = tys // CORES, txs
    tokens, part = x_ref.shape[1:]
    me_t, me_s = lax.axis_index("tx"), lax.axis_index("ty")
    my_x, my_c = me_s // CORES, lax.rem(me_s, CORES)
    sibling = my_x * CORES + (CORES - 1 - my_c)
    worker = me_t < each

    def ty_at(dx):
        return lax.rem(my_x + dx + nx, nx) * CORES + my_c

    def tx_at(dy):
        return lax.rem(me_t + dy + ny, ny)

    def target(to):
        if to == "sib":
            return {"ty": sibling}
        dx, dy = STEPS[to]
        return {"ty": ty_at(dx)} if dx else {"tx": tx_at(dy)}

    fills = [pltpu.make_async_copy(w, own_a.at[:, i], in_sem.at[i]) for i, w in enumerate((wq_ref, wk_ref, wv_ref, wo_ref))]
    fills += [pltpu.make_async_copy(wup_ref, own_u, in_sem.at[4]), pltpu.make_async_copy(wdown_ref, own_d, in_sem.at[5])]
    for c in fills:
        c.start()
    for i, ref in enumerate((gain1_ref, shift1_ref, bo_ref, gain2_ref, shift2_ref, bdown_ref)):
        own_vec[i] = ref[...]
    pair = o_ref.shape[1]
    own_bias[:, pl.ds(0, pair)] = jnp.concatenate([bq_ref[:, i, :] for i in range(pair // head)], axis=-1)
    own_bias[:, pl.ds(pair, pair)] = jnp.zeros((layers, pair), F32)
    own_bias[:, pl.ds(2 * pair, pair)] = jnp.concatenate([bv_ref[:, i, :] for i in range(pair // head)], axis=-1)
    own_bias[:, pl.ds(3 * pair, bup_ref.shape[1])] = bup_ref[...]

    barrier = pltpu.get_barrier_semaphore()
    for k in range(1, txs):
        pl.semaphore_signal(barrier, inc=1, device_id={"tx": tx_at(k)}, device_id_type=MESH)
    for k in range(1, tys):
        pl.semaphore_signal(barrier, inc=1, device_id={"ty": lax.rem(me_s + k, tys)}, device_id_type=MESH)
    pl.semaphore_wait(barrier, txs - 1 + tys - 1)

    def halves(g):
        cut = 1 if g == 0 else 2
        return {"all": pl.ds(0, 4), "A": pl.ds(0, cut), "B": pl.ds(cut, 4 - cut)}

    signs = {"all": pl.ds(0, 2), "plus": pl.ds(0, 1), "minus": pl.ds(1, 1)}

    def piece(g, ty, tx, half, sign):
        return gathered[g % 3].at[g // 3, ty, tx, halves(g)[half], signs[sign]]

    def copy(phase, i, g):
        to, (dx, dy), half, sign = PHASES[phase][i]
        place = piece(g, ty_at(dx), tx_at(dy), half, sign)
        return pltpu.make_async_remote_copy(
            src_ref=owns[g % 3].at[g // 3] if phase == 0 else place, dst_ref=place, send_sem=send_sem.at[g % 3, phase],
            recv_sem=core_sem.at[g, abs(dx)] if to == "sib" else recv_sem.at[g, phase],
            device_id=target(to), device_id_type=MESH)

    def wait_all(place, sem):
        pltpu.make_async_copy(place, place, sem).wait()

    def blocks(g, shape):
        return gathered[g % 3].at[g // 3, pl.ds(0, shape[0]), pl.ds(0, shape[1])]

    def column(step):
        rem = lax.rem if isinstance(step, jax.Array) else lambda p, q: p % q
        region = (step // 2 + 1) // 2
        near = rem(region, 2)
        ring = near * (1 + rem(step, 2)) + 3 * (region // 2)
        core = (1 - near) * rem(step, 2) + near * (step // 2 - 1)
        return lax.rem(my_x + ring + ring // 2 - 2 * (ring // 3), nx) * CORES + lax.rem(my_c + core, CORES)

    def load(k, layer, step):
        return pltpu.make_async_copy(gathered[k].at[layer, column(step)], (wbuf_a, wbuf_u, wbuf_d)[k].at[step], load_sem.at[k, step])

    def event(kind, first, second):
        with jax.named_scope(f"{kind}_{first}_{second}"):
            first, second = int(first), int(second)
            if kind == "c":
                wait_all(blocks(first, PASSED[second]), core_sem.at[first, second])
            if kind in "cl":
                @pl.when(worker)
                def _():
                    for step in RINGS[second][kind == "c"]:
                        load(first % 3, first // 3, step).start()
                return
            phase, g = first, second
            if phase:
                wait_all(blocks(g, BROUGHT[phase - 1]), recv_sem.at[g, phase - 1])
            for i in range(len(PHASES[phase])):
                copy(phase, i, g).start()

    for c in fills[:4]:
        c.wait()
    event("s", 0, 0)
    for c in fills[4:]:
        c.wait()
    keep = [pltpu.make_async_copy(owns[i], gathered[i].at[:, me_s, me_t], own_sem.at[i]) for i in range(3)]
    for c in keep:
        c.start()

    def x_copy(j):
        return pltpu.make_async_remote_copy(
            src_ref=x_hbm.at[me_s * each + j], dst_ref=x_ref.at[me_t], send_sem=xin_send,
            recv_sem=xin_recv.at[me_t], device_id={"tx": j}, device_id_type=MESH)

    def x_local():
        return pltpu.make_async_copy(x_hbm.at[me_s * each + me_t], x_ref.at[me_t], xin_recv.at[me_t])

    for j in range(each):
        @pl.when(me_t != j)
        def _():
            x_copy(j).start()

        @pl.when(me_t == j)
        def _():
            x_local().start()

    def vec_copy(k):
        return pltpu.make_async_remote_copy(
            src_ref=own_vec, dst_ref=vecs.at[me_t], send_sem=vec_send, recv_sem=vec_recv,
            device_id={"tx": tx_at(k)}, device_id_type=MESH)

    def bias_copy(k):
        return pltpu.make_async_remote_copy(
            src_ref=own_bias, dst_ref=biases.at[me_s], send_sem=bias_send, recv_sem=bias_recv,
            device_id={"ty": lax.rem(me_s + k, tys)}, device_id_type=MESH)

    for k in range(1, txs):
        vec_copy(k).start()
    for k in range(1, tys):
        bias_copy(k).start()
    vecs[me_t] = own_vec[...]
    biases[me_s] = own_bias[...]

    for e in BEFORE.split():
        event(*e)

    with jax.named_scope("wait_vectors"):
        for sem in (vec_send, vec_recv):
            wait_all(vecs.at[pl.ds(0, txs - 1)], sem)
        for sem in (bias_send, bias_recv):
            wait_all(biases.at[pl.ds(0, tys - 1)], sem)
        for c in keep:
            c.wait()

    @pl.when(worker)
    def _():
        with jax.named_scope("wait_x"):
            for m in range(txs):
                pltpu.make_async_copy(x_hbm.at[0], x_ref.at[m], xin_recv.at[m]).wait()

    def vec(row, layer):
        return jnp.concatenate([vecs[t, row, pl.ds(layer, 1), :] for t in range(txs)], axis=-1)

    def norm(gain_row, shift_row, layer):
        rows = 96

        def body(r, _):
            at = pl.ds(pl.multiple_of(r * rows, rows), rows)
            x_f = jnp.concatenate([x_ref[t, at, :] for t in range(txs)], axis=-1).astype(F32)
            mean = jnp.mean(x_f, axis=-1, keepdims=True)
            centred = x_f - mean
            variance = jnp.mean(centred * centred, axis=-1, keepdims=True)
            h = (centred * lax.rsqrt(variance + EPS) * vec(gain_row, layer) + vec(shift_row, layer)).astype(BF16)
            for t in range(txs):
                h_ref[t, at, :] = h[:, t * part:(t + 1) * part]
                acc_ref[t, at, :] = jnp.zeros((rows, part), F32)
            return 0

        lax.fori_loop(0, tokens // rows, body, 0)

    def finish(bias_row, layer, start, count):
        rows = 48

        def body(r, _):
            at = pl.ds(pl.multiple_of(start + r * rows, rows), rows)
            for t in range(txs):
                bias = vecs[t, bias_row, pl.ds(layer, 1), :]
                x_ref[t, at, :] = (x_ref[t, at, :].astype(F32) + acc_ref[t, at, :] + bias).astype(BF16)
            return 0

        lax.fori_loop(0, count // rows, body, 0)

    def run(parts, kinds, layer, body, middle=None):
        def step_body(step, _):
            for s, names in enumerate(parts):
                @pl.when(step == s)
                def _(names=names):
                    for e in names.split():
                        event(*e)

            if middle is not None:
                @pl.when(step == tys // 2)
                def _():
                    middle()

            @pl.when(worker)
            def _():
                if parts:
                    with jax.named_scope("wait_load"):
                        for k in kinds:
                            load(k, layer, step).wait()
                with jax.named_scope(f"compute_{kinds[0]}_{layer}"):
                    body(column(step), step)
            return 0

        lax.fori_loop(0, tys, step_body, 0)

    def attention(layer, ty, slot):
        def project(first, columns):
            total = jnp.zeros((tokens, columns), F32)
            for t in range(txs):
                w = wbuf_a[slot, t, pl.ds(first, columns // pair)].reshape(columns, part)
                total += lax.dot_general(h_ref[t], w, (((1,), (1,)), ((), ())), preferred_element_type=F32)
            return total

        at = pl.ds(0, 2 * pair)
        qkv_ref[:, at] = (project(0, 2 * pair) + biases[ty, pl.ds(layer, 1), at]).astype(BF16)
        at = pl.ds(2 * pair, pair)
        qkv_ref[:, at] = (project(2, pair) + biases[ty, pl.ds(layer, 1), at]).astype(BF16)

        scale = head ** -0.5 * math.log2(math.e)
        chunk = 192
        for c in range(tokens // chunk):
            rows = pl.ds(c * chunk, chunk)
            outs = []
            for hd in range(pair // head):
                q = qkv_ref[rows, pl.ds(hd * head, head)]
                k = qkv_ref[:, pl.ds(pair + hd * head, head)]
                v = qkv_ref[:, pl.ds(2 * pair + hd * head, head)]
                s = lax.dot_general(q, k, (((1,), (1,)), ((), ())), preferred_element_type=F32)
                e = jnp.exp2((s - jnp.max(s, axis=-1, keepdims=True)) * scale)
                p = (e * (1.0 / jnp.sum(e, axis=-1, keepdims=True))).astype(BF16)
                outs.append(dot(p, v))
            o_ref[rows, :] = jnp.concatenate(outs, axis=-1).astype(BF16)

        for t in range(txs):
            acc_ref[t] += dot(o_ref[...], wbuf_a[slot, t, 3].reshape(pair, part))

    def mlp(layer, start, count, ty, slot):
        rows = pl.ds(start, count)
        hidden = u_ref.shape[1]
        for n in range(hidden // part):
            at = pl.ds(n * part, part)
            total = jnp.zeros((count, part), F32)
            for t in range(txs):
                total += dot(h_ref[t, rows, :], wbuf_u[slot, t, :, :, :, at].reshape(part, part))
            bias = biases[ty, pl.ds(layer, 1), pl.ds(3 * pair + n * part, part)]
            u_ref[rows, at] = jax.nn.gelu(total + bias, approximate=True).astype(BF16)
        for t in range(txs):
            acc_ref[t, rows, :] += dot(u_ref[rows, :], wbuf_d[slot, t].reshape(hidden, part))

    def at_work(scope, *calls):
        @pl.when(worker)
        def _():
            with jax.named_scope(scope):
                for f, *args in calls:
                    f(*args)

    each_part = tokens // PARTS
    for layer in range(layers):
        last = layer == layers - 1
        at_work("norm", (norm, 0, 1, layer))
        run(SLOTS[2 * layer], (0,), layer, functools.partial(attention, layer))
        at_work("finish_norm", (finish, 2, layer, 0, tokens), (norm, 3, 4, layer))
        if not last:
            run(SLOTS[2 * layer + 1], (1, 2), layer, functools.partial(mlp, layer, 0, tokens))
            at_work("finish", (finish, 5, layer, 0, tokens))

    def o1_copy(j, r):
        rows = pl.ds(r * each_part, each_part)
        return pltpu.make_async_remote_copy(
            src_ref=x_ref.at[j, rows], dst_ref=out_ref.at[me_s * each + me_t, rows], send_sem=o1_send,
            recv_sem=o1_recv.at[r, me_t], device_id={"tx": j}, device_id_type=MESH)

    def slices(r):
        @pl.when(worker)
        def _():
            for j in reversed(range(txs)):
                @pl.when(me_t != j)
                def _(j=j):
                    o1_copy(j, r).start()

    def keep_own(r):
        rows = pl.ds(r * each_part, each_part)
        out_ref[me_s * each + me_t, rows, :] = x_ref[me_t, rows, :]

    def part_of(image, r):
        return out_ref.at[image, pl.ds(r * each_part, each_part)]

    def wait_slice(m, r):
        wait_all(part_of(0, r), o1_recv.at[r, m])

    ring = (("xp", 0, 0, 2), ("xm", 0, 0, 2), ("sib", 0, 0, 2),
            ("xp", -1, 0, 1), ("xm", 1, 1, 1), ("sib", -1, 0, 2), ("sib", 1, 0, 2), ("sib", 2, 0, 2))

    def ring_place(kind, ty, m, r):
        first, count = ring[kind][2:]
        return out_ref.at[ty * each + m, pl.ds(r * each_part + first * each_part // 2, count * each_part // 2)]

    def ring_copy(kind, m, r):
        to, dx, _, count = ring[kind]
        place = ring_place(kind, ty_at(dx), m, r)
        if to == "sib":
            sem = ring_core
        else:
            sem = ring_recv.at[2 if count == 1 else kind, r * each + m]
        return pltpu.make_async_remote_copy(
            src_ref=place, dst_ref=place, send_sem=ring_send.at[kind], recv_sem=sem, device_id=target(to), device_id_type=MESH)

    def ring_wait(stage, m, r):
        wait_all(part_of(0, r), ring_recv.at[stage, r * each + m])

    def start_ring(m, r):
        for kind in (0, 1, 2):
            ring_copy(kind, m, r).start()

    def mlp_part(r, middle):
        run(SLOTS[2 * layers - 1] if r == 0 else (), (1, 2), layers - 1,
            functools.partial(mlp, layers - 1, r * each_part, each_part), middle)
        at_work("finish", (finish, 5, layers - 1, r * each_part, each_part))

        @pl.when(worker)
        def _():
            keep_own(r)
        slices(r)

        @pl.when(worker)
        def _():
            start_ring(me_t, r)

    def spread(m, r):
        @pl.when(me_t != m)
        def _():
            wait_slice(m, r)
            start_ring(m, r)

    def pass_on(m, r):
        ring_wait(0, m, r)
        ring_copy(3, m, r).start()
        ring_copy(5, m, r).start()
        ring_wait(1, m, r)
        ring_copy(4, m, r).start()
        ring_copy(6, m, r).start()

    def hand_over(m, r):
        ring_wait(2, m, r)
        ring_copy(7, m, r).start()

    def stages(r):
        def each_image(*todo):
            todo = [(stage, r - delay) for stage, delay in todo if 0 <= r - delay < PARTS]

            def body(i, _):
                for stage, of in todo:
                    stage(lax.rem(me_t + i, each), of)
                return 0

            if todo:
                lax.fori_loop(0, each, body, 0)

        with jax.named_scope(f"output_{r}"):
            each_image((pass_on, 2), (spread, 1))
            each_image((hand_over, 3))

    for r in range(PARTS):
        mlp_part(r, functools.partial(stages, r) if r else None)
    for r in range(PARTS, PARTS + 3):
        stages(r)

    with jax.named_scope("wait_core"):
        wait_all(out_ref.at[pl.ds(0, 4 * each)], ring_core)

    with jax.named_scope("wait_sent"):
        for kind in range(len(ring)):
            wait_all(out_ref.at[pl.ds(0, each), pl.ds(0, tokens * ring[kind][3] // 2)], ring_send.at[kind])

        @pl.when(worker)
        def _():
            wait_all(x_hbm.at[pl.ds(0, each - 1)], xin_send)
            wait_all(x_ref.at[pl.ds(0, txs - 1)], o1_send)

        @pl.when(jnp.logical_not(worker))
        def _():
            wait_all(x_hbm.at[pl.ds(0, each)], xin_send)
        for k in range(3):
            for phase, (a, b) in enumerate(SENT):
                wait_all(gathered[k].at[:, pl.ds(0, a), pl.ds(0, b)], send_sem.at[k, phase])


def solution(mesh):
    txs, tys = mesh.shape["tx"], mesh.shape["ty"]
    act_spec = P("dp", None, "tx")
    vec_tx = P(None, "tx")
    proj_spec = P(None, "tx", "ty", None)
    head_vec = P(None, "ty", None)
    in_specs = (act_spec, vec_tx, vec_tx, proj_spec, head_vec, proj_spec, proj_spec, head_vec,
                P(None, "ty", None, "tx"), vec_tx, vec_tx, vec_tx,
                P(None, "tx", "ty"), P(None, "ty"), P(None, "ty", "tx"), vec_tx)

    def local_fn(x_in, ln1_gain, ln1_bias, w_q, b_q, w_k, w_v, b_v, w_o, b_o, ln2_gain, ln2_bias, w_up, b_up, w_down, b_down):
        layers, depth, heads, head = w_q.shape
        imgs, tokens, part = x_in.shape
        hidden = w_up.shape[2]
        each, pair = imgs // tys, heads * head
        assert tys == 4 * CORES and txs == 4 and 4 * pair == hidden and depth == part and hidden % part == 0 and each < txs

        tall, wide = (4, 2, hidden // 8, part), (4, 2, depth // 8, hidden)
        wq, wk, wv = (w.transpose(0, 2, 3, 1).reshape((layers,) + tall[1:]) for w in (w_q, w_k, w_v))
        wo = w_o.reshape((layers,) + tall[1:])

        vmem = pl.BlockSpec(memory_space=pltpu.VMEM)
        hbm = pl.BlockSpec(memory_space=pl.ANY)
        dma = pltpu.SemaphoreType.DMA

        def buf(lead, shape):
            return pltpu.VMEM(lead + shape, BF16)

        out, *_ = pl.pallas_call(
            functools.partial(kernel, head, each),
            out_shape=(pltpu.VMEM(x_in.shape, BF16),
                       jax.ShapeDtypeStruct((layers, tys, txs) + tall, BF16),
                       jax.ShapeDtypeStruct((layers, tys, txs) + wide, BF16),
                       jax.ShapeDtypeStruct((layers, tys, txs) + tall, BF16)),
            in_specs=[hbm] * 7 + [vmem] * 9,
            out_specs=(vmem,) + (hbm,) * 3,
            scratch_shapes=[
                buf((txs,), (tokens, part)), buf((txs,), (tokens, part)), pltpu.VMEM((txs, tokens, part), F32),
                buf((), (tokens, 3 * pair)), buf((), (tokens, pair)), buf((), (tokens, hidden)),
                buf((layers,), tall), buf((layers,), wide), buf((layers,), tall),
                buf((tys, txs), tall), buf((tys, txs), wide), buf((tys, txs), tall),
                pltpu.VMEM((6, layers, part), F32), pltpu.VMEM((layers, 3 * pair + hidden), F32),
                pltpu.VMEM((txs, 6, layers, part), F32), pltpu.VMEM((tys, layers, 3 * pair + hidden), F32),
                dma((3, 5)), dma((3 * layers, 4)), dma((3 * layers, 3)), dma((6,)), dma((3,)), dma((3, tys)), dma, dma, dma, dma,
                dma, dma((txs,)), dma, dma((PARTS, txs)), dma((8,)), dma((3, PARTS * each)), dma,
            ],
            compiler_params=pltpu.CompilerParams(collective_id=0, has_side_effects=True, vmem_limit_bytes=52 << 20),
            cost_estimate=pl.CostEstimate(flops=80_000_000_000, bytes_accessed=150_000_000, transcendentals=20_000_000),
            name="encoder",
        )(x_in, wq, wk, wv, wo, w_up.reshape((layers,) + wide), w_down.reshape((layers,) + tall),
          b_q, b_v, b_up, ln1_gain, ln1_bias, b_o, ln2_gain, ln2_bias, b_down)
        return out

    return jax.shard_map(local_fn, mesh=mesh, in_specs=in_specs, out_specs=act_spec, check_vma=False)
```

profile of v0, /device:TPU:97, one launch (start us, length us, event | category | flops | bytes accessed | tf_op | source)
XLA Modules:
  0.0 196.1 jit_solution(7150535156560326654)
XLA Ops:
  0.0 193.2 %encoder.1 = (bf16[24,576,256]{2,1,0:T(8,128)(2,1)S(1)}, bf16[2,8,4,4,2,64,256]{6,5,4,3,2,1,0:T(8,128)(2,1)}, bf16[2,8,4,4,2,32,512]{6,5,4,3,2,1,0:T(8,128)(2,1)}, bf16[2,8,4,4,2,64,256]{6,5,4,3,2,1,0:T(8,128)(2,1)}) custom-call(bf16[24,576,256]{2,1,0:T(8,128)(2,1)} %x_hbm.1, bf16[2,2,64,256]{3,2,1,0:T(8,128)(2,1)} %bitcast.7, ...), custom_call_target="tpu_custom_call" | custom-call | flops 80000000000 | bytes 150000000 | tf_op jit(solution)/shard_map/encoder/pallas_call | solution.py:485
  193.2 3.0 %copy.18 = bf16[24,576,256]{2,1,0:T(8,128)(2,1)} copy(bf16[24,576,256]{2,1,0:T(8,128)(2,1)S(1)} %get-tuple-element.6) | data formatting | bytes 14155776
where the time goes:
time: 196 us
  Pallas kernels  193 us (98%)
  local copies, waits for them, and re-layouts  2.96 us (2%)
    pallas_call x1, Pallas kernels, local_fn(): pl.pallas_call(functools.partial(kernel, head, each), out_shape=(pltpu.VM...  193 us

commit v1 on v0

--- a/solution.py
+++ b/solution.py
@@ -49,7 +49,7 @@
     ("s35 l51 s44 l42", "c41 c51", "s45 l52", "", "", "", "c42 c52", ""),
 )
 RINGS = (((0,), (1,)), ((2, 3), (4, 5)), ((6,), (7,)))
-PARTS = 4
+PARTS = 3
 
 
 def dot(a, b):
@@ -236,7 +236,7 @@
         lax.fori_loop(0, tokens // rows, body, 0)
 
     def finish(bias_row, layer, start, count):
-        rows = 48
+        rows = 96
 
         def body(r, _):
             at = pl.ds(pl.multiple_of(start + r * rows, rows), rows)
@@ -342,10 +342,13 @@
     def slices(r):
         @pl.when(worker)
         def _():
-            for j in reversed(range(txs)):
-                @pl.when(me_t != j)
-                def _(j=j):
-                    o1_copy(j, r).start()
+            for far in (False, True):
+                for j in reversed(range(txs)):
+                    is_far = lax.rem(me_t - j + txs, txs) == txs // 2
+
+                    @pl.when((me_t != j) & (is_far if far else jnp.logical_not(is_far)))
+                    def _(j=j):
+                        o1_copy(j, r).start()
 
     def keep_own(r):
         rows = pl.ds(r * each_part, each_part)
@@ -419,7 +422,7 @@
 
             def body(i, _):
                 for stage, of in todo:
-                    stage(lax.rem(me_t + i, each), of)
+                    stage(lax.rem(me_t + (each - 1) * i, each), of)
                 return 0
 
             if todo:

time: 196 us -> 196 us (level)
  no operation moved by 1% of the time
where the time goes in v1:
time: 196 us
  Pallas kernels  193 us (98%)
  local copies, waits for them, and re-layouts  2.96 us (2%)
    pallas_call x1, Pallas kernels, local_fn(): pl.pallas_call(functools.partial(kernel, head, each), out_shape=(pltpu.VM...  193 us

profile of v1, /device:TPU:97, one launch (start us, length us, event | category | flops | bytes accessed | tf_op | source)
XLA Modules:
  0.0 196.2 jit_solution(317922740854420497)
XLA Ops:
  0.0 193.2 %encoder.1 = (bf16[24,576,256]{2,1,0:T(8,128)(2,1)S(1)}, bf16[2,8,4,4,2,64,256]{6,5,4,3,2,1,0:T(8,128)(2,1)}, bf16[2,8,4,4,2,32,512]{6,5,4,3,2,1,0:T(8,128)(2,1)}, bf16[2,8,4,4,2,64,256]{6,5,4,3,2,1,0:T(8,128)(2,1)}) custom-call(bf16[24,576,256]{2,1,0:T(8,128)(2,1)} %x_hbm.1, bf16[2,2,64,256]{3,2,1,0:T(8,128)(2,1)} %bitcast.7, ...), custom_call_target="tpu_custom_call" | custom-call | flops 80000000000 | bytes 150000000 | tf_op jit(solution)/shard_map/encoder/pallas_call | solution.py:488
  193.2 3.0 %copy.18 = bf16[24,576,256]{2,1,0:T(8,128)(2,1)} copy(bf16[24,576,256]{2,1,0:T(8,128)(2,1)S(1)} %get-tuple-element.6) | data formatting | bytes 14155776
